TPU v7x, 256 devices: a 4x2x16 block of a 4x16x16 slice. The times are simulated.
256 devices in a mesh: groups: 2 (over y), expert: 4 (over x), etp: 32 (over z, core).
Axes of the slice: x: 4, y: 2, z: 16, core: 2. Of those that a mesh axis runs over, the one named last changes fastest.
The devices are a block of a 4x16x16 slice.
Arguments:
- tokens: bfloat16 [1024, 4096], P(('groups', 'expert'), 'etp'), parts along dimension 0, may hold values from -6 to 6
- route_ids: int32 [1024, 2], P(('groups', 'expert')), parts along dimension 0, may hold values from 0 to 3, all different within a row; in each aligned block of 128 rows (0 to 127, 128 to 255, ...) at most 96 rows name the same one
- gate_weights: float32 [1024, 2], P(('groups', 'expert')), parts along dimension 0, may hold values from 0.2 to 1
- w_gate: bfloat16 [4, 4096, 14336], P('expert', None, 'etp'), may hold values from -0.09375 to 0.09375
- w_up: bfloat16 [4, 4096, 14336], P('expert', None, 'etp'), may hold values from -0.09375 to 0.09375
- w_down: bfloat16 [4, 14336, 4096], P('expert', 'etp'), may hold values from -0.09375 to 0.09375
Outputs:
- mixed: bfloat16 [1024, 4096], P(('groups', 'expert'), 'etp'), parts along dimension 0
There are 2 independent parts, one for each index of `groups`. A program takes and returns all parts, laid end to end along the dimension named above; an argument that names none is the same for every part. Nothing has to cross between parts.
Inputs may be any that keep to these rules, and one draw needn't show every extreme that they name: `route_ids`: each row names two different experts. In the rows of one index of expert (128 aligned rows), no expert is named by more than 96 rows, a bound that some block reaches.
All inputs are finite; a program needn't handle non-finite values.
Results may differ from a plain program's by a relative error of at most 0.024.
Values may be sent and summed in bfloat16 or wider, within the bound.
No kernel may reach another device: no remote copies, remote signals or barrier semaphores. Data moves between devices by JAX's collectives and lax.ppermute only.
A program may use at most 64 MiB of HBM per device.

v0:
```python
import jax
import jax.numpy as jnp
from jax import lax
from jax.sharding import Mesh
from jax.sharding import PartitionSpec as P

CAP = 96
ETP = ("etp_0", "etp_1")


def joined_along(tiles, dim):
    shape = list(tiles.shape[1:])
    shape[dim] *= tiles.shape[0]
    return jnp.moveaxis(tiles, 0, dim).reshape(shape)


def all_blocks(shard, axes, order):
    tiles = shard[None]
    for k in order:
        tiles = lax.all_gather(tiles, axes[k], axis=0, tiled=True)
    current = [lax.axis_size(axes[k]) for k in reversed(order)]
    tiles = tiles.reshape(*current, *shard.shape)
    turned = sorted(range(len(order)), key=lambda place: order[len(order) - 1 - place])
    return tiles.transpose(*turned, *range(len(order), tiles.ndim)).reshape(-1, *shard.shape)


def whole_of(shard, axes, order, dim):
    return joined_along(all_blocks(shard, axes, order), dim)


def cut_along(shard, dim, count):
    shape = shard.shape
    tiles = shard.reshape(*shape[:dim], count, shape[dim] // count, *shape[dim + 1 :])
    return jnp.moveaxis(tiles, dim, 0)


def sum_at_owner(shard, axis, dim):
    tiles = cut_along(shard, dim, lax.axis_size(axis))
    arrived = lax.all_to_all(tiles, axis, split_axis=0, concat_axis=0, tiled=True)
    return arrived.astype(jnp.float32).sum(axis=0)


def shards(tokens, route_ids, gate_weights, w_gate, w_up, w_down):
    cycle_size = lax.axis_size("expert")
    token_count, local_width = tokens.shape
    slot_total = cycle_size * CAP
    expert_iota = lax.broadcasted_iota(jnp.int32, (1, 1, cycle_size), 2)
    hit_mask = route_ids[:, :, None] == expert_iota
    routed = jnp.any(hit_mask, axis=1).astype(jnp.int32)
    weighting = jnp.sum(jnp.where(hit_mask, gate_weights[:, :, None], 0.0), axis=1)
    slot_index = jnp.cumsum(routed, axis=0) - 1
    expert_base = lax.broadcasted_iota(jnp.int32, (1, cycle_size), 1) * CAP
    target_slot = jnp.where(routed == 1, expert_base + slot_index, -1)
    slot_iota = lax.broadcasted_iota(jnp.int32, (1, 1, slot_total), 2)
    pick_table = target_slot[:, :, None] == slot_iota
    select_table = jnp.any(pick_table, axis=1).astype(jnp.bfloat16)
    combine_table = jnp.sum(jnp.where(pick_table, weighting[:, :, None], 0.0), axis=1)
    dispatched = jnp.dot(select_table.T, tokens, preferred_element_type=jnp.float32)
    dispatched = dispatched.astype(jnp.bfloat16).reshape(cycle_size, CAP, local_width)
    gate_local = w_gate[0]
    up_local = w_up[0]
    down_local = w_down[0]
    received = lax.all_to_all(dispatched, "expert", split_axis=0, concat_axis=0, tiled=True)
    columns_in = whole_of(received.reshape(slot_total, local_width), ETP, (0, 1), 1)
    gate_sum = jnp.dot(columns_in, gate_local, preferred_element_type=jnp.float32)
    up_sum = jnp.dot(columns_in, up_local, preferred_element_type=jnp.float32)
    hidden = (jax.nn.silu(gate_sum) * up_sum).astype(jnp.bfloat16)
    partial_out = jnp.dot(hidden, down_local, preferred_element_type=jnp.float32).astype(
        jnp.bfloat16
    )
    finished = sum_at_owner(partial_out, ETP, 1).astype(jnp.bfloat16)
    results = lax.all_to_all(
        finished.reshape(cycle_size, CAP, local_width),
        "expert",
        split_axis=0,
        concat_axis=0,
        tiled=True,
    )
    flat_results = results.reshape(slot_total, local_width).astype(jnp.float32)
    mixed = jnp.dot(combine_table, flat_results)
    return mixed.astype(jnp.bfloat16)


def solution(mesh):
    finer = Mesh(
        mesh.devices.reshape(mesh.shape["groups"], mesh.shape["expert"], 16, 2),
        ("groups", "expert", "etp_0", "etp_1"),
    )
    placed = (
        P(("groups", "expert"), ETP),
        P(("groups", "expert"), None),
        P(("groups", "expert"), None),
        P("expert", None, ETP),
        P("expert", None, ETP),
        P("expert", ETP, None),
    )
    return jax.shard_map(
        shards, mesh=finer, in_specs=placed, out_specs=P(("groups", "expert"), ETP), check_vma=False
    )
```

profile of v0, /device:TPU:160, one launch (start us, length us, event | category | flops | bytes accessed | tf_op | source)
XLA Modules:
  0.0 320.1 jit_solution(13523252470046150234)
XLA Ops:
  6.5 0.0 copy-start
  6.6 0.0 all-gather.3.cloned.1.call-start
  6.6 0.7 fusion.18
  7.3 0.1 copy.29
  7.4 0.2 reduce_window_sum.11
  7.6 0.1 copy.30
  7.6 0.1 add_select_fusion
  7.7 0.2 fusion.14
  7.9 0.0 copy-done
  7.9 0.3 convolution_convert_fusion.1
  8.1 10.3 %all_to_all.15 = bf16[4,96,128]{2,1,0:T(8,128)(2,1)} all-to-all(bf16[4,96,128]{2,1,0:T(8,128)(2,1)S(1)} %bitcast.49), channel_id=1, replica_groups=mesh['groups'=2,'expert'=4,'etp_0'=16,'etp_1'=2] {'expert'}, dimensions={0} | all-to-all | bytes 196608 | tf_op jit(solution)/shard_map/all_to_all | solution.py:63
  18.4 0.1 all-gather.3.cloned.1.call-update
  18.5 0.1 all-gather.5.cloned.1.call-start
  18.6 80.5 %all-gather.3.cloned.1.call-done = bf16[16,384,128]{2,1,0:T(8,128)(2,1)} async-done(((bf16[1,384,128]{2,1,0:T(8,128)(2,1)}), bf16[16,384,128]{2,1,0:T(8,128)(2,1)}) %all-gather.3.cloned.1.call-update) | async-done | bytes 1572880 | tf_op jit(solution)/shard_map/all_gather | solution.py:20
  99.1 0.1 all-gather.5.cloned.1.call-update
  99.1 19.8 %all-gather.5.cloned.1.call-done = bf16[32,384,128]{2,1,0:T(8,128)(2,1)} async-done(((bf16[16,384,128]{2,1,0:T(8,128)(2,1)}), bf16[32,384,128]{2,1,0:T(8,128)(2,1)}) %all-gather.5.cloned.1.call-update) | async-done | bytes 3145744 | tf_op jit(solution)/shard_map/all_gather | solution.py:20
  119.0 2.1 copy.31
  121.1 2.8 copy.32
  123.9 0.0 copy-start.1
  123.9 6.0 %fusion.3 = f32[384,448]{0,1:T(8,128)} fusion(bf16[384,4096]{0,1:T(8,128)(2,1)} %bitcast.45, bf16[1,4096,448]{1,2,0:T(8,128)(2,1)} %param.9), kind=kOutput, calls=%fused_computation.4 | convolution fusion | flops 1409286144 | bytes 7503872 | tf_op jit(solution)/shard_map/dot_general | solution.py:65
  130.0 0.0 copy-done.1
  130.0 8.9 %fusion.5 = bf16[48,32,8,128]{3,2,1,0:T(8,128)(2,1)} fusion(bf16[1,448,4096]{2,1,0:T(8,128)(2,1)} %param.11, bf16[384,4096]{0,1:T(8,128)(2,1)S(1)} %bitcast.46, bf16[1,4096,448]{1,2,0:T(8,128)(2,1)} %param.10, f32[384,448]{0,1:T(8,128)} %fusion.3), kind=kOutput, calls=%fused_computation.7 | convolution fusion | flops 2821177344 | bytes 14319616 | tf_op jit(solution)/shard_map/dot_general | solution.py:68
  138.8 4.5 %copy.36 = bf16[48,32,8,128]{3,2,0,1:T(8,128)(2,1)} copy(bf16[48,32,8,128]{3,2,1,0:T(8,128)(2,1)} %fusion.5) | data formatting | bytes 6291456 | tf_op jit(solution)/shard_map/reshape | solution.py:33
  143.3 0.0 copy-start.2
  143.3 0.0 copy-start.3
  143.3 13.0 %all-to-all-start.1 = ((bf16[32,384,128]{2,1,0:T(8,128)(2,1)}), bf16[32,384,128]{2,1,0:T(8,128)(2,1)S(1)}, u32[]{:S(2)}, u32[]{:S(2)}) async-start(bf16[32,384,128]{2,1,0:T(8,128)(2,1)} %bitcast.42), calls=%async_computation.1 | async-start | bytes 6291456 | tf_op jit(solution)/shard_map/all_to_all | solution.py:39
  156.4 0.0 copy-done.2
  156.4 0.0 copy-done.3
  156.4 144.9 %all-to-all-done.1 = bf16[32,384,128]{2,1,0:T(8,128)(2,1)S(1)} async-done(((bf16[32,384,128]{2,1,0:T(8,128)(2,1)}), bf16[32,384,128]{2,1,0:T(8,128)(2,1)S(1)}, u32[]{:S(2)}, u32[]{:S(2)}) %all-to-all-start.1) | async-done | bytes 3145760 | tf_op jit(solution)/shard_map/all_to_all | solution.py:39
  301.3 1.1 reduce_sum.32
  302.4 4.3 %all-to-all-start.2 = ((bf16[4,96,128]{2,1,0:T(8,128)(2,1)}), bf16[4,96,128]{2,1,0:T(8,128)(2,1)S(1)}, u32[]{:S(2)}, u32[]{:S(2)}) async-start(bf16[4,96,128]{2,1,0:T(8,128)(2,1)} %bitcast.11), calls=%async_computation.2 | async-start | bytes 196608 | tf_op jit(solution)/shard_map/all_to_all | solution.py:72
  306.7 0.2 select_reduce_fusion
  306.9 5.6 %all-to-all-done.2 = bf16[4,96,128]{2,1,0:T(8,128)(2,1)S(1)} async-done(((bf16[4,96,128]{2,1,0:T(8,128)(2,1)}), bf16[4,96,128]{2,1,0:T(8,128)(2,1)S(1)}, u32[]{:S(2)}, u32[]{:S(2)}) %all-to-all-start.2) | async-done | bytes 98336 | tf_op jit(solution)/shard_map/all_to_all | solution.py:72
  312.5 0.8 fusion.20
  (3 shorter events, 0.0 us)
Async XLA Ops:
  6.5 1.3 copy-start
  6.6 92.5 %all-gather.3.cloned.1.call-start = ((), (), s32[]{:S(2)}) async-start(), calls=%async_computation.3 | async-start | bytes 1671168 | tf_op jit(solution)/shard_map/all_gather | solution.py:20
  18.5 100.5 %all-gather.5.cloned.1.call-start = ((), (), s32[]{:S(2)}) async-start(), calls=%async_computation.4 | async-start | bytes 4718592 | tf_op jit(solution)/shard_map/all_gather | solution.py:20
  123.9 6.0 %copy-start.1 = (bf16[384,32,128]{0,2,1:T(8,128)(2,1)S(1)}, bf16[384,32,128]{0,2,1:T(8,128)(2,1)}, u32[]{:S(2)}) copy-start(bf16[384,32,128]{0,2,1:T(8,128)(2,1)} %copy.32) | copy-start | bytes 9437188
  143.3 13.1 %copy-start.2 = (f32[128,2]{0,1:T(2,128)S(1)}, f32[128,2]{0,1:T(2,128)}, u32[]{:S(2)}) copy-start(f32[128,2]{0,1:T(2,128)} %param.8) | copy-start | bytes 3076
  143.3 13.1 %copy-start.3 = (s32[128,2]{0,1:T(2,128)S(1)}, s32[128,2]{0,1:T(2,128)}, u32[]{:S(2)}) copy-start(s32[128,2]{0,1:T(2,128)} %param.7) | copy-start | bytes 3076
  143.3 158.0 %all-to-all-start.1 = ((bf16[32,384,128]{2,1,0:T(8,128)(2,1)}), bf16[32,384,128]{2,1,0:T(8,128)(2,1)S(1)}, u32[]{:S(2)}, u32[]{:S(2)}) async-start(bf16[32,384,128]{2,1,0:T(8,128)(2,1)} %bitcast.42), calls=%async_computation.1 | async-start | bytes 6291456 | tf_op jit(solution)/shard_map/all_to_all | solution.py:39
  302.4 10.1 %all-to-all-start.2 = ((bf16[4,96,128]{2,1,0:T(8,128)(2,1)}), bf16[4,96,128]{2,1,0:T(8,128)(2,1)S(1)}, u32[]{:S(2)}, u32[]{:S(2)}) async-start(bf16[4,96,128]{2,1,0:T(8,128)(2,1)} %bitcast.11), calls=%async_computation.2 | async-start | bytes 196608 | tf_op jit(solution)/shard_map/all_to_all | solution.py:72
Sparse Core Ops, SparseCore 0:
  18.6 80.4 all-gather.2
  100.9 18.0 all-gather.4
where the time goes:
time: 321 us; the launch traced here: 320 us
  waiting for transfers between devices  251 us (78%)
  starting transfers between devices  17.4 us (5%)
  matrix products  16 us (5%)
  between operations  13.5 us (4%)
  blocking collectives  10.3 us (3%)
  local copies, waits for them, and re-layouts  9.57 us (3%)
    all_to_all x1, waiting for transfers between devices, sum_at_owner(): lax.all_to_all(tiles, axis, split_axis=0, concat_axis=0, tiled=True)  145 us
    all_gather x2, waiting for transfers between devices, all_blocks(): tiles = lax.all_gather(tiles, axes[k], axis=0, tiled=True)  100 us
    all_to_all x1, starting transfers between devices, sum_at_owner(): lax.all_to_all(tiles, axis, split_axis=0, concat_axis=0, tiled=True)  13 us
    all_to_all x1, blocking collectives, shards(): lax.all_to_all(dispatched, 'expert', split_axis=0, concat_axis=0, tiled=T...  10.3 us
    dot_general x1, matrix products, shards(): jnp.dot(hidden, down_local, preferred_element_type=jnp.float32)  8.87 us
  transfers between devices with their start and end apart: 4, of which 4 were waited for; matrix products, arithmetic and copies ran while one was open for 0% of the time, Pallas kernels for 0%

commit v1 on v0

--- a/solution.py
+++ b/solution.py
@@ -3,6 +3,7 @@
 from jax import lax
 from jax.sharding import Mesh
 from jax.sharding import PartitionSpec as P
+from jax.lax import all_to_all, psum
 
 CAP = 96
 ETP = ("etp_0", "etp_1")
@@ -17,7 +18,16 @@
 def all_blocks(shard, axes, order):
     tiles = shard[None]
     for k in order:
-        tiles = lax.all_gather(tiles, axes[k], axis=0, tiled=True)
+        panel = axes[k]
+        tiles = jnp.concatenate(
+            all_to_all(
+                jnp.stack([tiles for _ in range(psum(1, axis_name=panel))], 0),
+                split_axis=0,
+                concat_axis=0,
+                axis_name=panel,
+            ),
+            0,
+        )
     current = [lax.axis_size(axes[k]) for k in reversed(order)]
     tiles = tiles.reshape(*current, *shard.shape)
     turned = sorted(range(len(order)), key=lambda place: order[len(order) - 1 - place])

time: 321 us -> 300 us (0.935)
  waiting for transfers between devices: 251 us -> 150 us
  blocking collectives: 10.3 us -> 111 us
  between operations: 13.5 us -> 0.09 us
  starting transfers between devices: 17.4 us -> 10.6 us
    all_to_all x0 -> x2, blocking collectives: none -> 101 us  [all_blocks(): all_to_all(jnp.stack([tiles for _ in range(psum(1, axis_name=panel))], 0)...]
    all_gather x2 -> x0, waiting for transfers between devices: 100 us -> none  [all_blocks(): tiles = lax.all_gather(tiles, axes[k], axis=0, tiled=True)]
    all_to_all x1, starting transfers between devices: 13 us -> 7.19 us  [sum_at_owner(): lax.all_to_all(tiles, axis, split_axis=0, concat_axis=0, tiled=True)]
  transfers between devices with their start and end apart: 4 -> 2, of which waited for: 4 -> 2; matrix products, arithmetic and copies ran while one was open for 0% -> 0% of each run, Pallas kernels for 0% -> 0%
where the time goes in v1:
time: 300 us; the launch traced here: 299 us
  waiting for transfers between devices  150 us (50%)
  blocking collectives  111 us (37%)
  matrix products  16 us (5%)
  starting transfers between devices  10.6 us (4%)
  local copies, waits for them, and re-layouts  7.97 us (3%)
    all_to_all x1, waiting for transfers between devices, sum_at_owner(): lax.all_to_all(tiles, axis, split_axis=0, concat_axis=0, tiled=True)  145 us
    all_to_all x2, blocking collectives, all_blocks(): all_to_all(jnp.stack([tiles for _ in range(psum(1, axis_name=panel))], 0)...  101 us
    all_to_all x1, blocking collectives, shards(): lax.all_to_all(dispatched, 'expert', split_axis=0, concat_axis=0, tiled=T...  10.2 us
    dot_general x1, matrix products, shards(): jnp.dot(hidden, down_local, preferred_element_type=jnp.float32)  8.89 us
    all_to_all x1, starting transfers between devices, sum_at_owner(): lax.all_to_all(tiles, axis, split_axis=0, concat_axis=0, tiled=True)  7.19 us
    dot_general x1, matrix products, shards(): jnp.dot(columns_in, gate_local, preferred_element_type=jnp.float32)  6.05 us
  transfers between devices with their start and end apart: 2, of which 2 were waited for; matrix products, arithmetic and copies ran while one was open for 0% of the time, Pallas kernels for 0%

profile of v1, /device:TPU:160, one launch (start us, length us, event | category | flops | bytes accessed | tf_op | source)
XLA Modules:
  0.0 299.2 jit_solution(2593261359349848149)
XLA Ops:
  0.0 0.0 copy-start
  0.0 0.7 fusion.18
  0.7 0.1 copy.25
  0.8 0.2 reduce_window_sum.11
  1.0 0.1 copy.26
  1.1 0.1 add_select_fusion
  1.1 0.2 fusion.14
  1.3 0.0 copy-done
  1.3 0.3 convolution_convert_fusion.1
  1.6 10.2 %all_to_all.25 = bf16[4,96,128]{2,1,0:T(8,128)(2,1)S(1)} all-to-all(bf16[4,96,128]{2,1,0:T(8,128)(2,1)S(1)} %bitcast.49), channel_id=1, replica_groups=mesh['groups'=2,'expert'=4,'etp_0'=16,'etp_1'=2] {'expert'}, dimensions={0} | all-to-all | bytes 196608 | tf_op jit(solution)/shard_map/all_to_all | solution.py:73
  11.8 0.3 stack.6
  12.1 95.0 %all_to_all.26 = bf16[16,1,384,128]{3,2,1,0:T(8,128)(2,1)S(1)} all-to-all(bf16[16,1,384,128]{3,2,1,0:T(8,128)(2,1)S(1)} %stack.6), channel_id=1, replica_groups=mesh['groups'=2,'expert'=4,'etp_0'=16,'etp_1'=2] {'etp_0'}, dimensions={0} | all-to-all | bytes 3145728 | tf_op jit(solution)/shard_map/all_to_all | solution.py:23
  107.1 0.3 pad_maximum_fusion
  107.4 6.3 %all_to_all.27 = bf16[2,16,384,128]{3,2,1,0:T(8,128)(2,1)S(1)} all-to-all(bf16[2,16,384,128]{3,2,1,0:T(8,128)(2,1)S(1)} %pad_maximum_fusion), channel_id=1, replica_groups=mesh['groups'=2,'expert'=4,'etp_0'=16,'etp_1'=2] {'etp_1'}, dimensions={0} | all-to-all | bytes 6291456 | tf_op jit(solution)/shard_map/all_to_all | solution.py:23
  113.6 0.2 copy.27
  113.9 2.8 copy.28
  116.7 0.0 copy-start.1
  116.7 6.1 %fusion.3 = f32[384,448]{0,1:T(8,128)} fusion(bf16[384,4096]{0,1:T(8,128)(2,1)} %bitcast.45, bf16[1,4096,448]{1,2,0:T(8,128)(2,1)} %param.9), kind=kOutput, calls=%fused_computation.4 | convolution fusion | flops 1409286144 | bytes 7503872 | tf_op jit(solution)/shard_map/dot_general | solution.py:75
  122.7 0.0 copy-done.1
  122.7 8.9 %fusion.5 = bf16[48,32,8,128]{3,2,1,0:T(8,128)(2,1)} fusion(bf16[1,448,4096]{2,1,0:T(8,128)(2,1)} %param.11, bf16[384,4096]{0,1:T(8,128)(2,1)S(1)} %bitcast.46, bf16[1,4096,448]{1,2,0:T(8,128)(2,1)} %param.10, f32[384,448]{0,1:T(8,128)} %fusion.3), kind=kOutput, calls=%fused_computation.8 | convolution fusion | flops 2821177344 | bytes 14319616 | tf_op jit(solution)/shard_map/dot_general | solution.py:78
  131.6 4.5 %copy.32 = bf16[48,32,8,128]{3,2,0,1:T(8,128)(2,1)} copy(bf16[48,32,8,128]{3,2,1,0:T(8,128)(2,1)} %fusion.5) | data formatting | bytes 6291456 | tf_op jit(solution)/shard_map/reshape | solution.py:43
  136.1 0.0 copy-start.2
  136.1 0.0 copy-start.3
  136.1 7.2 %all-to-all-start.3 = ((bf16[32,384,128]{2,1,0:T(8,128)(2,1)}), bf16[32,384,128]{2,1,0:T(8,128)(2,1)S(1)}, u32[]{:S(2)}, u32[]{:S(2)}) async-start(bf16[32,384,128]{2,1,0:T(8,128)(2,1)} %bitcast.42), calls=%async_computation.3 | async-start | bytes 6291456 | tf_op jit(solution)/shard_map/all_to_all | solution.py:49
  143.3 0.0 copy-done.2
  143.3 0.0 copy-done.3
  143.3 144.9 %all-to-all-done.3 = bf16[32,384,128]{2,1,0:T(8,128)(2,1)S(1)} async-done(((bf16[32,384,128]{2,1,0:T(8,128)(2,1)}), bf16[32,384,128]{2,1,0:T(8,128)(2,1)S(1)}, u32[]{:S(2)}, u32[]{:S(2)}) %all-to-all-start.3) | async-done | bytes 3145760 | tf_op jit(solution)/shard_map/all_to_all | solution.py:49
  288.2 1.1 reduce_sum.32
  289.3 3.4 %all-to-all-start.4 = ((bf16[4,96,128]{2,1,0:T(8,128)(2,1)}), bf16[4,96,128]{2,1,0:T(8,128)(2,1)S(1)}, u32[]{:S(2)}, u32[]{:S(2)}) async-start(bf16[4,96,128]{2,1,0:T(8,128)(2,1)} %bitcast.11), calls=%async_computation.4 | async-start | bytes 196608 | tf_op jit(solution)/shard_map/all_to_all | solution.py:82
  292.7 0.2 select_reduce_fusion
  292.9 5.5 %all-to-all-done.4 = bf16[4,96,128]{2,1,0:T(8,128)(2,1)S(1)} async-done(((bf16[4,96,128]{2,1,0:T(8,128)(2,1)}), bf16[4,96,128]{2,1,0:T(8,128)(2,1)S(1)}, u32[]{:S(2)}, u32[]{:S(2)}) %all-to-all-start.4) | async-done | bytes 98336 | tf_op jit(solution)/shard_map/all_to_all | solution.py:82
  298.4 0.8 fusion.20
  (3 shorter events, 0.0 us)
Async XLA Ops:
  0.0 1.3 copy-start
  116.7 6.1 %copy-start.1 = (bf16[384,32,128]{0,2,1:T(8,128)(2,1)S(1)}, bf16[384,32,128]{0,2,1:T(8,128)(2,1)}, u32[]{:S(2)}) copy-start(bf16[384,32,128]{0,2,1:T(8,128)(2,1)} %copy.28) | copy-start | bytes 9437188
  136.1 7.2 %copy-start.2 = (f32[128,2]{0,1:T(2,128)S(1)}, f32[128,2]{0,1:T(2,128)}, u32[]{:S(2)}) copy-start(f32[128,2]{0,1:T(2,128)} %param.8) | copy-start | bytes 3076
  136.1 7.2 %copy-start.3 = (s32[128,2]{0,1:T(2,128)S(1)}, s32[128,2]{0,1:T(2,128)}, u32[]{:S(2)}) copy-start(s32[128,2]{0,1:T(2,128)} %param.7) | copy-start | bytes 3076
  136.1 152.2 %all-to-all-start.3 = ((bf16[32,384,128]{2,1,0:T(8,128)(2,1)}), bf16[32,384,128]{2,1,0:T(8,128)(2,1)S(1)}, u32[]{:S(2)}, u32[]{:S(2)}) async-start(bf16[32,384,128]{2,1,0:T(8,128)(2,1)} %bitcast.42), calls=%async_computation.3 | async-start | bytes 6291456 | tf_op jit(solution)/shard_map/all_to_all | solution.py:49
  289.3 9.1 %all-to-all-start.4 = ((bf16[4,96,128]{2,1,0:T(8,128)(2,1)}), bf16[4,96,128]{2,1,0:T(8,128)(2,1)S(1)}, u32[]{:S(2)}, u32[]{:S(2)}) async-start(bf16[4,96,128]{2,1,0:T(8,128)(2,1)} %bitcast.11), calls=%async_computation.4 | async-start | bytes 196608 | tf_op jit(solution)/shard_map/all_to_all | solution.py:82
